TPU v7x, 1024 devices: a whole 4x8x16 slice. The times are simulated.
1024 devices in a mesh: dp: 64 (over x, y, core), tensor: 16 (over z).
Axes of the slice: x: 4, y: 8, z: 16, core: 2. Of those that a mesh axis runs over, the one named last changes fastest.
Arguments:
- tokens: bfloat16 [8192, 6144], P('dp', 'tensor'), may hold values from -6 to 6
- expert_ids: int32 [8192, 2], P('dp'), may hold values from 0 to 63, all different within a row; in each aligned block of 128 rows (0 to 127, 128 to 255, ...) at most 5 rows name the same one
- combine: float32 [8192, 2], P('dp'), may hold values from 0.2 to 1
- up_weight: bfloat16 [64, 6144, 2048], P('dp', None, 'tensor'), may hold values from -0.078125 to 0.078125
- down_weight: bfloat16 [64, 2048, 6144], P('dp', 'tensor'), may hold values from -0.1875 to 0.1875
Outputs:
- mixed: bfloat16 [8192, 6144], P('dp', 'tensor')
Inputs may be any that keep to these rules, and one draw needn't show every extreme that they name: `expert_ids`: each token names 2 different experts. Among the 128 tokens of one index of dp, no expert is named more than 5 times, a bound that some block reaches.
All inputs are finite; a program needn't handle non-finite values.
Results may differ from a plain program's by a relative error of at most 0.019.
Values may be sent and summed in bfloat16 or wider, within the bound.
No kernel may reach another device: no remote copies, remote signals or barrier semaphores. Data moves between devices by JAX's collectives and lax.ppermute only.
A program may use at most 32 MiB of HBM per device.

v0:
```python
import jax
import jax.numpy as jnp
from jax import lax
from jax.experimental.layout import Layout, with_layout_constraint
from jax.sharding import PartitionSpec as P


LANES = 128
SCALE = 8192.0


GROUPS = 4


def shift(value, step):
    size = lax.axis_size("tensor")
    return lax.ppermute(value, "tensor", [(i, (i + step) % size) for i in range(size)])


def leap(value):
    size = lax.axis_size("tensor")
    pairs = [(i, (i + (2 if i % 2 else -2)) % size) for i in range(size)]
    return lax.ppermute(value, "tensor", pairs)


def on_device(tokens, expert_ids, combine, up_weight, down_weight):
    tok_rows, feat = tokens.shape
    experts = lax.axis_size("dp")
    places = lax.axis_size("tensor")
    stride = places // GROUPS
    capacity = 5 * tok_rows // (2 * experts)
    picks = expert_ids.shape[1]
    tiles = feat // LANES
    packed_rows = -(-(capacity * tiles) // 16) * 16
    row_count = experts * capacity

    down_local = down_weight[0]
    mine = lax.axis_index("tensor")

    down_late = lax.optimization_barrier(down_local)

    def share(source, move):
        cuts = []
        for turn in range(GROUPS):
            owner = (mine + move + turn * stride + places) % places
            cuts.append(lax.dynamic_slice_in_dim(source, owner * feat, feat, axis=1))
        block = jnp.concatenate(cuts, axis=1)
        return with_layout_constraint(block, Layout(major_to_minor=(0, 1)))

    leapt = leap(share(down_local, jnp.where(mine % 2 == 0, -2, 2)))
    down_parts = [share(down_late, 0)]
    down_parts += [shift(share(down_late, move), move) for move in (1, -1)]
    down_parts.append(leapt)

    token = jnp.arange(tok_rows, dtype=jnp.int32)
    before = token[:, None] < token[None, :]
    slots = []
    for pick in range(picks):
        same = jnp.zeros((tok_rows, tok_rows), jnp.int32)
        for other in range(picks):
            same = same + (expert_ids[:, other][:, None] == expert_ids[:, pick][None, :])
        slots.append(jnp.sum(jnp.where(before, same, 0), axis=0))
    slots = jnp.stack(slots, axis=1)
    place = expert_ids * packed_rows + slots
    spots = jnp.arange(experts * packed_rows, dtype=jnp.int32)[None, :]

    def chosen(pick, tile):
        return place[:, pick][:, None] + tile * capacity == spots

    both = jnp.concatenate([chosen(0, tile) | chosen(1, tile) for tile in range(tiles)], axis=0)
    stacked = jnp.concatenate(
        [tokens[:, tile * LANES : (tile + 1) * LANES] for tile in range(tiles)], axis=0
    )
    outgoing = jnp.einsum(
        "ts,tf->sf", both.astype(jnp.bfloat16), stacked, preferred_element_type=jnp.float32
    )
    outgoing = outgoing.astype(jnp.bfloat16).reshape(experts, packed_rows, LANES)
    received = lax.all_to_all(outgoing, "dp", split_axis=0, concat_axis=0, tiled=True)
    received = received.reshape(experts * packed_rows, LANES)

    rows = jnp.arange(row_count, dtype=jnp.int32)
    row_spot = (rows // capacity) * packed_rows + rows % capacity

    row_spots = jnp.concatenate([row_spot + tile * capacity for tile in range(tiles)])
    unpacker = (row_spots[:, None] == spots).astype(jnp.bfloat16)
    flat_rows = jnp.dot(unpacker, received, preferred_element_type=jnp.float32)
    flat_rows = jnp.concatenate(
        [flat_rows[tile * row_count : (tile + 1) * row_count] for tile in range(tiles)], axis=1
    )
    scaled = (flat_rows * SCALE).astype(jnp.float16)
    gathered = lax.all_gather(scaled, "tensor", axis=1, tiled=True)
    accum = jnp.dot(gathered.astype(jnp.bfloat16), up_weight[0], preferred_element_type=jnp.float32)
    hidden = jax.nn.silu(accum * (1.0 / SCALE)).astype(jnp.bfloat16)
    pieces = [hidden, shift(hidden, 1), shift(hidden, -1), leap(hidden)]
    hidden = jnp.concatenate(pieces, axis=1)
    down_mine = jnp.concatenate(down_parts, axis=0)

    def block(k):
        columns = down_mine[:, k * feat : (k + 1) * feat]
        return jnp.dot(hidden, columns, preferred_element_type=jnp.float32)

    half = row_count // 2
    across = block(2).astype(jnp.bfloat16)
    far_one = shift(across[:half], stride)
    far_two = shift(across[half:], -stride)
    ahead, behind = block(1), block(3)
    near_one = shift(ahead[half:].astype(jnp.bfloat16), stride)
    near_two = shift(behind[:half].astype(jnp.bfloat16), -stride)
    keep = block(0)
    sum_one = shift((ahead[:half] + far_one.astype(jnp.float32)).astype(jnp.bfloat16), stride)
    sum_two = shift((behind[half:] + far_two.astype(jnp.float32)).astype(jnp.bfloat16), -stride)
    upper = keep[:half] + near_two.astype(jnp.float32) + sum_one.astype(jnp.float32)
    lower = keep[half:] + near_one.astype(jnp.float32) + sum_two.astype(jnp.float32)
    result = jnp.concatenate([upper, lower], axis=0).astype(jnp.bfloat16)

    stacked = jnp.concatenate(
        [result[:, tile * LANES : (tile + 1) * LANES] for tile in range(tiles)], axis=0
    )
    spot = jnp.arange(experts * packed_rows, dtype=jnp.int32)
    within = spot % packed_rows
    source_row = within // capacity * row_count + spot // packed_rows * capacity + within % capacity
    source_row = jnp.where(within < tiles * capacity, source_row, -1)
    packer = source_row[:, None] == jnp.arange(tiles * row_count, dtype=jnp.int32)[None, :]
    packed = jnp.dot(packer.astype(jnp.bfloat16), stacked, preferred_element_type=jnp.float32)
    packed = packed.astype(jnp.bfloat16).reshape(experts, packed_rows, LANES)
    returned = lax.all_to_all(packed, "dp", split_axis=0, concat_axis=0, tiled=True)
    returned = returned.reshape(experts * packed_rows, LANES)
    spread = jnp.concatenate(
        [jnp.roll(returned, -tile * capacity, axis=0) for tile in range(tiles)], axis=1
    )
    total = 0.0
    for pick in range(picks):
        one_hot = chosen(pick, 0).astype(jnp.bfloat16)
        row = jnp.dot(one_hot, spread, preferred_element_type=jnp.float32)
        total = total + row * combine[:, pick][:, None]
    return with_layout_constraint(total.astype(jnp.bfloat16), Layout(major_to_minor=(0, 1)))


def solution(mesh):
    placed = (
        P("dp", "tensor"),
        P("dp", None),
        P("dp", None),
        P("dp", None, "tensor"),
        P("dp", "tensor", None),
    )
    return jax.shard_map(
        on_device, mesh=mesh, in_specs=placed, out_specs=P("dp", "tensor"), check_vma=False
    )
```

profile of v0, /device:TPU:1, one launch (start us, length us, event | category | flops | bytes accessed | tf_op | source)
XLA Modules:
  0.0 191.1 jit_solution(16982414069363718801)
XLA Ops:
  0.0 1.6 constant_dynamic-slice_fusion.11
  1.7 4.8 %collective-permute-start.3 = (bf16[128,1536]{1,0:T(8,128)(2,1)S(1)}, bf16[128,1536]{1,0:T(8,128)(2,1)S(1)}, u32[]{:S(2)}, u32[]{:S(2)}) collective-permute-start(bf16[128,1536]{1,0:T(8,128)(2,1)S(1)} %pad_maximum_fusion.1), channel_id=1, source_target_pairs={{0,1},{1,2},{2,3},{3,4},{4,5},{5,6},{6,7},{7,8},{8,9},{9,10},{10,1... | collective-permute-start | bytes 1179656 | tf_op jit(solution)/shard_map/ppermute | solution.py:17
  6.5 0.8 pad_maximum_fusion.2
  7.3 15.9 %collective-permute-start.4 = (bf16[128,1536]{1,0:T(8,128)(2,1)}, bf16[128,1536]{1,0:T(8,128)(2,1)S(1)}, u32[]{:S(2)}, u32[]{:S(2)}) collective-permute-start(bf16[128,1536]{1,0:T(8,128)(2,1)} %pad_maximum_fusion.2), channel_id=1, source_target_pairs={{0,15},{1,0},{2,1},{3,2},{4,3},{5,4},{6,5},{7,6},{8,7},{9,8},{10,9... | collective-permute-start | bytes 1179656 | tf_op jit(solution)/shard_map/ppermute | solution.py:17
  23.8 1.3 fusion.13
  25.1 11.3 %all-to-all-start = ((bf16[64,16,128]{2,1,0:T(8,128)(2,1)}), bf16[64,16,128]{2,1,0:T(8,128)(2,1)}, u32[]{:S(2)}, u32[]{:S(2)}) async-start(bf16[64,16,128]{2,1,0:T(8,128)(2,1)} %bitcast.10), calls=%async_computation | async-start | bytes 524288 | tf_op jit(solution)/shard_map/all_to_all | solution.py:78
  36.5 1.1 dynamic-slice_bitcast_fusion.3
  37.5 0.8 pad_maximum_fusion.3
  38.3 3.6 %collective-permute-start.5 = (bf16[128,1536]{1,0:T(8,128)(2,1)}, bf16[128,1536]{1,0:T(8,128)(2,1)S(1)}, u32[]{:S(2)}, u32[]{:S(2)}) collective-permute-start(bf16[128,1536]{1,0:T(8,128)(2,1)} %pad_maximum_fusion.3), channel_id=1, source_target_pairs={{0,14},{1,3},{2,0},{3,5},{4,2},{5,7},{6,4},{7,9},{8,6},{9,11},{10,... | collective-permute-start | bytes 1179656 | tf_op jit(solution)/shard_map/ppermute | solution.py:23
  42.1 6.2 %all-to-all-done = bf16[64,16,128]{2,1,0:T(8,128)(2,1)} async-done(((bf16[64,16,128]{2,1,0:T(8,128)(2,1)}), bf16[64,16,128]{2,1,0:T(8,128)(2,1)}, u32[]{:S(2)}, u32[]{:S(2)}) %all-to-all-start) | async-done | bytes 262176 | tf_op jit(solution)/shard_map/all_to_all | solution.py:78
  48.3 1.7 fusion.3
  50.1 51.4 %all-gather.1 = f16[320,6144]{1,0:T(8,128)(2,1)S(1)} all-gather(f16[320,384]{1,0:T(8,128)(2,1)S(1)} %fusion.27), channel_id=1, replica_groups=mesh['dp'=64,'tensor'=16] {'tensor'}, dimensions={1}, use_global_device_ids=true | all-gather | bytes 4177920 | tf_op jit(solution)/shard_map/all_gather | solution.py:91
  101.5 1.2 multiply_convert_fusion
  102.7 3.7 %collective-permute-start = (bf16[320,128]{1,0:T(8,128)(2,1)S(1)}, bf16[320,128]{1,0:T(8,128)(2,1)S(1)}, u32[]{:S(2)}, u32[]{:S(2)}) collective-permute-start(bf16[320,128]{1,0:T(8,128)(2,1)S(1)} %multiply_convert_fusion), channel_id=1, source_target_pairs={{0,1},{1,2},{2,3},{3,4},{4,5},{5,6},{6,7},{7,8},{8,9},{9,10},{10,1... | collective-permute-start | bytes 245768 | tf_op jit(solution)/shard_map/ppermute | solution.py:17
  106.4 2.8 %collective-permute-start.1 = (bf16[320,128]{1,0:T(8,128)(2,1)S(1)}, bf16[320,128]{1,0:T(8,128)(2,1)S(1)}, u32[]{:S(2)}, u32[]{:S(2)}) collective-permute-start(bf16[320,128]{1,0:T(8,128)(2,1)S(1)} %multiply_convert_fusion), channel_id=1, source_target_pairs={{0,15},{1,0},{2,1},{3,2},{4,3},{5,4},{6,5},{7,6},{8,7},{9,8},{10,9... | collective-permute-start | bytes 245768 | tf_op jit(solution)/shard_map/ppermute | solution.py:17
  109.2 2.2 %collective-permute-start.2 = (bf16[320,128]{1,0:T(8,128)(2,1)S(1)}, bf16[320,128]{1,0:T(8,128)(2,1)S(1)}, u32[]{:S(2)}, u32[]{:S(2)}) collective-permute-start(bf16[320,128]{1,0:T(8,128)(2,1)S(1)} %multiply_convert_fusion), channel_id=1, source_target_pairs={{0,14},{1,3},{2,0},{3,5},{4,2},{5,7},{6,4},{7,9},{8,6},{9,11},{10,... | collective-permute-start | bytes 245768 | tf_op jit(solution)/shard_map/ppermute | solution.py:23
  111.4 2.4 %pad_maximum_fusion = bf16[512,1536]{1,0:T(8,128)(2,1)S(1)} fusion(bf16[128,1536]{1,0:T(8,128)(2,1)S(1)} %collective-permute-done.5, bf16[128,1536]{1,0:T(8,128)(2,1)S(1)} %collective-permute-done.4, bf16[128,1536]{1,0:T(8,128)(2,1)S(1)} %collective-permute-done.3, bf16[128,384]{1,0:T(8,128)(2,1)S(1)} %get-tuple-element.16, ...), kind=kLoop, calls=%fused_computation.8 | loop fusion | flops 11010048 | bytes 3145728 | tf_op jit(solution)/shard_map/concatenate | solution.py:96
  113.9 1.4 collective-permute-done.2
  115.7 5.3 %collective-permute-start.10 = (bf16[160,384]{1,0:T(8,128)(2,1)S(1)}, bf16[160,384]{1,0:T(8,128)(2,1)S(1)}, u32[]{:S(2)}, u32[]{:S(2)}) collective-permute-start(bf16[160,384]{1,0:T(8,128)(2,1)S(1)} %get-tuple-element.31), channel_id=1, source_target_pairs={{0,12},{1,13},{2,14},{3,15},{4,0},{5,1},{6,2},{7,3},{8,4},{9,5},{1... | collective-permute-start | bytes 368648 | tf_op jit(solution)/shard_map/ppermute | solution.py:17
  121.3 3.1 %collective-permute-start.6 = (bf16[160,384]{1,0:T(8,128)(2,1)S(1)}, bf16[160,384]{1,0:T(8,128)(2,1)S(1)}, u32[]{:S(2)}, u32[]{:S(2)}) collective-permute-start(bf16[160,384]{1,0:T(8,128)(2,1)S(1)} %slice.214), channel_id=1, source_target_pairs={{0,12},{1,13},{2,14},{3,15},{4,0},{5,1},{6,2},{7,3},{8,4},{9,5},{1... | collective-permute-start | bytes 368648 | tf_op jit(solution)/shard_map/ppermute | solution.py:17
  124.4 6.1 %collective-permute-start.7 = (bf16[160,384]{1,0:T(8,128)(2,1)S(1)}, bf16[160,384]{1,0:T(8,128)(2,1)S(1)}, u32[]{:S(2)}, u32[]{:S(2)}) collective-permute-start(bf16[160,384]{1,0:T(8,128)(2,1)S(1)} %get-tuple-element.30), channel_id=1, source_target_pairs={{0,4},{1,5},{2,6},{3,7},{4,8},{5,9},{6,10},{7,11},{8,12},{9,13},{1... | collective-permute-start | bytes 368648 | tf_op jit(solution)/shard_map/ppermute | solution.py:17
  130.9 3.9 %collective-permute-start.9 = (bf16[160,384]{1,0:T(8,128)(2,1)S(1)}, bf16[160,384]{1,0:T(8,128)(2,1)S(1)}, u32[]{:S(2)}, u32[]{:S(2)}) collective-permute-start(bf16[160,384]{1,0:T(8,128)(2,1)S(1)} %slice.213), channel_id=1, source_target_pairs={{0,4},{1,5},{2,6},{3,7},{4,8},{5,9},{6,10},{7,11},{8,12},{9,13},{1... | collective-permute-start | bytes 368648 | tf_op jit(solution)/shard_map/ppermute | solution.py:17
  134.9 5.3 %collective-permute-start.11 = (bf16[160,384]{1,0:T(8,128)(2,1)S(1)}, bf16[160,384]{1,0:T(8,128)(2,1)S(1)}, u32[]{:S(2)}, u32[]{:S(2)}) collective-permute-start(bf16[160,384]{1,0:T(8,128)(2,1)S(1)} %fusion.40), channel_id=1, source_target_pairs={{0,12},{1,13},{2,14},{3,15},{4,0},{5,1},{6,2},{7,3},{8,4},{9,5},{1... | collective-permute-start | bytes 368648 | tf_op jit(solution)/shard_map/ppermute | solution.py:17
  140.2 3.9 %collective-permute-start.8 = (bf16[160,384]{1,0:T(8,128)(2,1)S(1)}, bf16[160,384]{1,0:T(8,128)(2,1)S(1)}, u32[]{:S(2)}, u32[]{:S(2)}) collective-permute-start(bf16[160,384]{1,0:T(8,128)(2,1)S(1)} %fusion.43), channel_id=1, source_target_pairs={{0,4},{1,5},{2,6},{3,7},{4,8},{5,9},{6,10},{7,11},{8,12},{9,13},{1... | collective-permute-start | bytes 368648 | tf_op jit(solution)/shard_map/ppermute | solution.py:17
  144.1 0.3 fusion.33
  144.5 12.5 %collective-permute-done.9 = bf16[160,384]{1,0:T(8,128)(2,1)S(1)} collective-permute-done((bf16[160,384]{1,0:T(8,128)(2,1)S(1)}, bf16[160,384]{1,0:T(8,128)(2,1)S(1)}, u32[]{:S(2)}, u32[]{:S(2)}) %collective-permute-start.9) | collective-permute-done | bytes 122912 | tf_op jit(solution)/shard_map/ppermute | solution.py:17
  157.0 6.0 %collective-permute-done.8 = bf16[160,384]{1,0:T(8,128)(2,1)S(1)} collective-permute-done((bf16[160,384]{1,0:T(8,128)(2,1)S(1)}, bf16[160,384]{1,0:T(8,128)(2,1)S(1)}, u32[]{:S(2)}, u32[]{:S(2)}) %collective-permute-start.8) | collective-permute-done | bytes 122912 | tf_op jit(solution)/shard_map/ppermute | solution.py:17
  163.1 1.5 fusion.16
  164.6 13.0 %all-to-all-start.1 = ((bf16[64,16,128]{2,1,0:T(8,128)(2,1)}), bf16[64,16,128]{2,1,0:T(8,128)(2,1)S(1)}, u32[]{:S(2)}, u32[]{:S(2)}) async-start(bf16[64,16,128]{2,1,0:T(8,128)(2,1)} %bitcast.18), calls=%async_computation.1 | async-start | bytes 524288 | tf_op jit(solution)/shard_map/all_to_all | solution.py:126
  177.6 11.9 %all-to-all-done.1 = bf16[64,16,128]{2,1,0:T(8,128)(2,1)S(1)} async-done(((bf16[64,16,128]{2,1,0:T(8,128)(2,1)}), bf16[64,16,128]{2,1,0:T(8,128)(2,1)S(1)}, u32[]{:S(2)}, u32[]{:S(2)}) %all-to-all-start.1) | async-done | bytes 262176 | tf_op jit(solution)/shard_map/all_to_all | solution.py:126
  189.8 0.4 convolution_multiply_fusion
  190.1 1.0 fusion.18
  (46 shorter events, 2.2 us)
Async XLA Ops:
  0.0 101.5 %copy-start = (bf16[1,6144,128]{2,1,0:T(8,128)(2,1)S(1)}, bf16[1,6144,128]{2,1,0:T(8,128)(2,1)}, u32[]{:S(2)}) copy-start(bf16[1,6144,128]{2,1,0:T(8,128)(2,1)} %param.8) | copy-start | bytes 4718596
  0.0 23.2 %copy-start.2 = (s32[128,2]{0,1:T(2,128)S(1)}, s32[128,2]{0,1:T(2,128)}, u32[]{:S(2)}) copy-start(s32[128,2]{0,1:T(2,128)} %param.6) | copy-start | bytes 3076
  0.0 23.3 %copy-start.1 = (bf16[128,384]{1,0:T(8,128)(2,1)S(1)}, bf16[128,384]{1,0:T(8,128)(2,1)}, u32[]{:S(2)}) copy-start(bf16[128,384]{1,0:T(8,128)(2,1)} %param.5) | copy-start | bytes 294916
  1.7 107.5 %collective-permute-start.3 = (bf16[128,1536]{1,0:T(8,128)(2,1)S(1)}, bf16[128,1536]{1,0:T(8,128)(2,1)S(1)}, u32[]{:S(2)}, u32[]{:S(2)}) collective-permute-start(bf16[128,1536]{1,0:T(8,128)(2,1)S(1)} %pad_maximum_fusion.1), channel_id=1, source_target_pairs={{0,1},{1,2},{2,3},{3,4},{4,5},{5,6},{6,7},{7,8},{8,9},{9,10},{10,1... | collective-permute-start | bytes 1179656 | tf_op jit(solution)/shard_map/ppermute | solution.py:17
  7.3 104.1 %collective-permute-start.4 = (bf16[128,1536]{1,0:T(8,128)(2,1)}, bf16[128,1536]{1,0:T(8,128)(2,1)S(1)}, u32[]{:S(2)}, u32[]{:S(2)}) collective-permute-start(bf16[128,1536]{1,0:T(8,128)(2,1)} %pad_maximum_fusion.2), channel_id=1, source_target_pairs={{0,15},{1,0},{2,1},{3,2},{4,3},{5,4},{6,5},{7,6},{8,7},{9,8},{10,9... | collective-permute-start | bytes 1179656 | tf_op jit(solution)/shard_map/ppermute | solution.py:17
  25.1 23.2 %all-to-all-start = ((bf16[64,16,128]{2,1,0:T(8,128)(2,1)}), bf16[64,16,128]{2,1,0:T(8,128)(2,1)}, u32[]{:S(2)}, u32[]{:S(2)}) async-start(bf16[64,16,128]{2,1,0:T(8,128)(2,1)} %bitcast.10), calls=%async_computation | async-start | bytes 524288 | tf_op jit(solution)/shard_map/all_to_all | solution.py:78
  38.3 73.1 %collective-permute-start.5 = (bf16[128,1536]{1,0:T(8,128)(2,1)}, bf16[128,1536]{1,0:T(8,128)(2,1)S(1)}, u32[]{:S(2)}, u32[]{:S(2)}) collective-permute-start(bf16[128,1536]{1,0:T(8,128)(2,1)} %pad_maximum_fusion.3), channel_id=1, source_target_pairs={{0,14},{1,3},{2,0},{3,5},{4,2},{5,7},{6,4},{7,9},{8,6},{9,11},{10,... | collective-permute-start | bytes 1179656 | tf_op jit(solution)/shard_map/ppermute | solution.py:23
  102.7 11.2 %collective-permute-start = (bf16[320,128]{1,0:T(8,128)(2,1)S(1)}, bf16[320,128]{1,0:T(8,128)(2,1)S(1)}, u32[]{:S(2)}, u32[]{:S(2)}) collective-permute-start(bf16[320,128]{1,0:T(8,128)(2,1)S(1)} %multiply_convert_fusion), channel_id=1, source_target_pairs={{0,1},{1,2},{2,3},{3,4},{4,5},{5,6},{6,7},{7,8},{8,9},{9,10},{10,1... | collective-permute-start | bytes 245768 | tf_op jit(solution)/shard_map/ppermute | solution.py:17
  106.4 7.5 %collective-permute-start.1 = (bf16[320,128]{1,0:T(8,128)(2,1)S(1)}, bf16[320,128]{1,0:T(8,128)(2,1)S(1)}, u32[]{:S(2)}, u32[]{:S(2)}) collective-permute-start(bf16[320,128]{1,0:T(8,128)(2,1)S(1)} %multiply_convert_fusion), channel_id=1, source_target_pairs={{0,15},{1,0},{2,1},{3,2},{4,3},{5,4},{6,5},{7,6},{8,7},{9,8},{10,9... | collective-permute-start | bytes 245768 | tf_op jit(solution)/shard_map/ppermute | solution.py:17
  109.2 6.1 %collective-permute-start.2 = (bf16[320,128]{1,0:T(8,128)(2,1)S(1)}, bf16[320,128]{1,0:T(8,128)(2,1)S(1)}, u32[]{:S(2)}, u32[]{:S(2)}) collective-permute-start(bf16[320,128]{1,0:T(8,128)(2,1)S(1)} %multiply_convert_fusion), channel_id=1, source_target_pairs={{0,14},{1,3},{2,0},{3,5},{4,2},{5,7},{6,4},{7,9},{8,6},{9,11},{10,... | collective-permute-start | bytes 245768 | tf_op jit(solution)/shard_map/ppermute | solution.py:23
  115.7 19.1 %collective-permute-start.10 = (bf16[160,384]{1,0:T(8,128)(2,1)S(1)}, bf16[160,384]{1,0:T(8,128)(2,1)S(1)}, u32[]{:S(2)}, u32[]{:S(2)}) collective-permute-start(bf16[160,384]{1,0:T(8,128)(2,1)S(1)} %get-tuple-element.31), channel_id=1, source_target_pairs={{0,12},{1,13},{2,14},{3,15},{4,0},{5,1},{6,2},{7,3},{8,4},{9,5},{1... | collective-permute-start | bytes 368648 | tf_op jit(solution)/shard_map/ppermute | solution.py:17
  121.3 23.2 %collective-permute-start.6 = (bf16[160,384]{1,0:T(8,128)(2,1)S(1)}, bf16[160,384]{1,0:T(8,128)(2,1)S(1)}, u32[]{:S(2)}, u32[]{:S(2)}) collective-permute-start(bf16[160,384]{1,0:T(8,128)(2,1)S(1)} %slice.214), channel_id=1, source_target_pairs={{0,12},{1,13},{2,14},{3,15},{4,0},{5,1},{6,2},{7,3},{8,4},{9,5},{1... | collective-permute-start | bytes 368648 | tf_op jit(solution)/shard_map/ppermute | solution.py:17
  124.4 15.7 %collective-permute-start.7 = (bf16[160,384]{1,0:T(8,128)(2,1)S(1)}, bf16[160,384]{1,0:T(8,128)(2,1)S(1)}, u32[]{:S(2)}, u32[]{:S(2)}) collective-permute-start(bf16[160,384]{1,0:T(8,128)(2,1)S(1)} %get-tuple-element.30), channel_id=1, source_target_pairs={{0,4},{1,5},{2,6},{3,7},{4,8},{5,9},{6,10},{7,11},{8,12},{9,13},{1... | collective-permute-start | bytes 368648 | tf_op jit(solution)/shard_map/ppermute | solution.py:17
  130.9 26.1 %collective-permute-start.9 = (bf16[160,384]{1,0:T(8,128)(2,1)S(1)}, bf16[160,384]{1,0:T(8,128)(2,1)S(1)}, u32[]{:S(2)}, u32[]{:S(2)}) collective-permute-start(bf16[160,384]{1,0:T(8,128)(2,1)S(1)} %slice.213), channel_id=1, source_target_pairs={{0,4},{1,5},{2,6},{3,7},{4,8},{5,9},{6,10},{7,11},{8,12},{9,13},{1... | collective-permute-start | bytes 368648 | tf_op jit(solution)/shard_map/ppermute | solution.py:17
  134.9 22.1 %collective-permute-start.11 = (bf16[160,384]{1,0:T(8,128)(2,1)S(1)}, bf16[160,384]{1,0:T(8,128)(2,1)S(1)}, u32[]{:S(2)}, u32[]{:S(2)}) collective-permute-start(bf16[160,384]{1,0:T(8,128)(2,1)S(1)} %fusion.40), channel_id=1, source_target_pairs={{0,12},{1,13},{2,14},{3,15},{4,0},{5,1},{6,2},{7,3},{8,4},{9,5},{1... | collective-permute-start | bytes 368648 | tf_op jit(solution)/shard_map/ppermute | solution.py:17
  140.2 22.8 %collective-permute-start.8 = (bf16[160,384]{1,0:T(8,128)(2,1)S(1)}, bf16[160,384]{1,0:T(8,128)(2,1)S(1)}, u32[]{:S(2)}, u32[]{:S(2)}) collective-permute-start(bf16[160,384]{1,0:T(8,128)(2,1)S(1)} %fusion.43), channel_id=1, source_target_pairs={{0,4},{1,5},{2,6},{3,7},{4,8},{5,9},{6,10},{7,11},{8,12},{9,13},{1... | collective-permute-start | bytes 368648 | tf_op jit(solution)/shard_map/ppermute | solution.py:17
  163.0 14.6 %copy-start.3 = (f32[128,2]{0,1:T(2,128)S(1)}, f32[128,2]{0,1:T(2,128)}, u32[]{:S(2)}) copy-start(f32[128,2]{0,1:T(2,128)} %param.7) | copy-start | bytes 3076
  164.6 25.0 %all-to-all-start.1 = ((bf16[64,16,128]{2,1,0:T(8,128)(2,1)}), bf16[64,16,128]{2,1,0:T(8,128)(2,1)S(1)}, u32[]{:S(2)}, u32[]{:S(2)}) async-start(bf16[64,16,128]{2,1,0:T(8,128)(2,1)} %bitcast.18), calls=%async_computation.1 | async-start | bytes 524288 | tf_op jit(solution)/shard_map/all_to_all | solution.py:126
where the time goes:
time: 192 us; the launch traced here: 191 us
  starting transfers between devices  84.8 us (44%)
  blocking collectives  51.4 us (27%)
  waiting for transfers between devices  38.1 us (20%)
  matrix products  8.49 us (4%)
  other arithmetic  4.89 us (3%)
  local copies, waits for them, and re-layouts  3 us (2%)
    ppermute x10, starting transfers between devices, shift(): lax.ppermute(value, 'tensor', [(i, (i + step) % size) for i in range(size)])  54.7 us
    all_gather x1, blocking collectives, on_device(): gathered = lax.all_gather(scaled, 'tensor', axis=1, tiled=True)  51.4 us
    ppermute x10, waiting for transfers between devices, shift(): lax.ppermute(value, 'tensor', [(i, (i + step) % size) for i in range(size)])  18.5 us
    all_to_all x1, starting transfers between devices, on_device(): lax.all_to_all(packed, 'dp', split_axis=0, concat_axis=0, tiled=True)  13 us
    all_to_all x1, waiting for transfers between devices, on_device(): lax.all_to_all(packed, 'dp', split_axis=0, concat_axis=0, tiled=True)  11.9 us
    all_to_all x1, starting transfers between devices, on_device(): lax.all_to_all(outgoing, 'dp', split_axis=0, concat_axis=0, tiled=True)  11.3 us
    all_to_all x1, waiting for transfers between devices, on_device(): lax.all_to_all(outgoing, 'dp', split_axis=0, concat_axis=0, tiled=True)  6.19 us
    ppermute x2, starting transfers between devices, leap(): return lax.ppermute(value, 'tensor', pairs)  5.8 us
  transfers between devices with their start and end apart: 14, of which 5 were waited for; matrix products, arithmetic and copies ran while one was open for 6% of the time, Pallas kernels for 0%

commit v1 on v0

--- a/solution.py
+++ b/solution.py
@@ -37,20 +37,16 @@
     down_local = down_weight[0]
     mine = lax.axis_index("tensor")
 
-    down_late = lax.optimization_barrier(down_local)
-
-    def share(source, move):
+    def share(move):
         cuts = []
         for turn in range(GROUPS):
             owner = (mine + move + turn * stride + places) % places
-            cuts.append(lax.dynamic_slice_in_dim(source, owner * feat, feat, axis=1))
+            cuts.append(lax.dynamic_slice_in_dim(down_local, owner * feat, feat, axis=1))
         block = jnp.concatenate(cuts, axis=1)
         return with_layout_constraint(block, Layout(major_to_minor=(0, 1)))
 
-    leapt = leap(share(down_local, jnp.where(mine % 2 == 0, -2, 2)))
-    down_parts = [share(down_late, 0)]
-    down_parts += [shift(share(down_late, move), move) for move in (1, -1)]
-    down_parts.append(leapt)
+    down_parts = [share(0), shift(share(1), 1), shift(share(-1), -1)]
+    down_parts.append(leap(share(jnp.where(mine % 2 == 0, -2, 2))))
 
     token = jnp.arange(tok_rows, dtype=jnp.int32)
     before = token[:, None] < token[None, :]
@@ -83,6 +79,7 @@
 
     row_spots = jnp.concatenate([row_spot + tile * capacity for tile in range(tiles)])
     unpacker = (row_spots[:, None] == spots).astype(jnp.bfloat16)
+    unpacker = lax.optimization_barrier(unpacker)
     flat_rows = jnp.dot(unpacker, received, preferred_element_type=jnp.float32)
     flat_rows = jnp.concatenate(
         [flat_rows[tile * row_count : (tile + 1) * row_count] for tile in range(tiles)], axis=1
@@ -121,7 +118,8 @@
     source_row = within // capacity * row_count + spot // packed_rows * capacity + within % capacity
     source_row = jnp.where(within < tiles * capacity, source_row, -1)
     packer = source_row[:, None] == jnp.arange(tiles * row_count, dtype=jnp.int32)[None, :]
-    packed = jnp.dot(packer.astype(jnp.bfloat16), stacked, preferred_element_type=jnp.float32)
+    packer = lax.optimization_barrier(packer.astype(jnp.bfloat16))
+    packed = jnp.dot(packer, stacked, preferred_element_type=jnp.float32)
     packed = packed.astype(jnp.bfloat16).reshape(experts, packed_rows, LANES)
     returned = lax.all_to_all(packed, "dp", split_axis=0, concat_axis=0, tiled=True)
     returned = returned.reshape(experts * packed_rows, LANES)

time: 192 us -> 195 us (1.016)
  other arithmetic: 4.89 us -> 8.85 us
  starting transfers between devices: 84.8 us -> 82.1 us
    all_to_all x1, waiting for transfers between devices: 6.19 us -> 9.6 us  [on_device(): lax.all_to_all(outgoing, 'dp', split_axis=0, concat_axis=0, tiled=True)]
    all_to_all x1, starting transfers between devices: 13 us -> 10.2 us  [on_device(): lax.all_to_all(packed, 'dp', split_axis=0, concat_axis=0, tiled=True)]
    convert_element_type x0 -> x2, other arithmetic: none -> 2.14 us  [the longest x1 1.75 us: on_device(): packer = lax.optimization_barrier(packer.astype(jnp.bfloat16))]
  transfers between devices with their start and end apart: 14 -> 14, of which waited for: 5 -> 5; matrix products, arithmetic and copies ran while one was open for 6% -> 7% of each run, Pallas kernels for 0% -> 0%
where the time goes in v1:
time: 195 us; the launch traced here: 194 us
  starting transfers between devices  82.1 us (42%)
  blocking collectives  51.8 us (27%)
  waiting for transfers between devices  39.7 us (20%)
  other arithmetic  8.85 us (5%)
  matrix products  8.29 us (4%)
  local copies, waits for them, and re-layouts  2.76 us (1%)
    ppermute x10, starting transfers between devices, shift(): lax.ppermute(value, 'tensor', [(i, (i + step) % size) for i in range(size)])  54.9 us
    all_gather x1, blocking collectives, on_device(): gathered = lax.all_gather(scaled, 'tensor', axis=1, tiled=True)  51.8 us
    ppermute x10, waiting for transfers between devices, shift(): lax.ppermute(value, 'tensor', [(i, (i + step) % size) for i in range(size)])  17.6 us
    all_to_all x1, waiting for transfers between devices, on_device(): lax.all_to_all(packed, 'dp', split_axis=0, concat_axis=0, tiled=True)  11.9 us
    all_to_all x1, starting transfers between devices, on_device(): lax.all_to_all(outgoing, 'dp', split_axis=0, concat_axis=0, tiled=True)  11.8 us
    all_to_all x1, starting transfers between devices, on_device(): lax.all_to_all(packed, 'dp', split_axis=0, concat_axis=0, tiled=True)  10.2 us
    all_to_all x1, waiting for transfers between devices, on_device(): lax.all_to_all(outgoing, 'dp', split_axis=0, concat_axis=0, tiled=True)  9.6 us
    ppermute x2, starting transfers between devices, leap(): return lax.ppermute(value, 'tensor', pairs)  5.26 us
  transfers between devices with their start and end apart: 14, of which 5 were waited for; matrix products, arithmetic and copies ran while one was open for 7% of the time, Pallas kernels for 0%

profile of v1, /device:TPU:1, one launch (start us, length us, event | category | flops | bytes accessed | tf_op | source)
XLA Modules:
  0.0 194.0 jit_solution(10449576275522872703)
XLA Ops:
  0.0 2.5 %dynamic-slice_bitcast_fusion.15 = (bf16[128,384]{1,0:T(8,128)(2,1)}, bf16[128,384]{1,0:T(8,128)(2,1)S(1)}, bf16[128,384]{1,0:T(8,128)(2,1)S(1)}, bf16[128,384]{...) fusion(bf16[1,128,6144]{2,1,0:T(8,128)(2,1)} %param.9, ...), kind=kLoop, calls=%fused_computation.90 | loop fusion | bytes 3145792 | tf_op jit(solution)/shard_map/dynamic_slice | solution.py:44
  2.5 0.8 pad_maximum_fusion.1
  3.3 4.8 %collective-permute-start.3 = (bf16[128,1536]{1,0:T(8,128)(2,1)}, bf16[128,1536]{1,0:T(8,128)(2,1)}, u32[]{:S(2)}, u32[]{:S(2)}) collective-permute-start(bf16[128,1536]{1,0:T(8,128)(2,1)} %pad_maximum_fusion.1), channel_id=1, source_target_pairs={{0,1},{1,2},{2,3},{3,4},{4,5},{5,6},{6,7},{7,8},{8,9},{9,10},{10,1... | collective-permute-start | bytes 1179656 | tf_op jit(solution)/shard_map/ppermute | solution.py:17
  8.1 0.8 pad_maximum_fusion.2
  8.9 15.9 %collective-permute-start.4 = (bf16[128,1536]{1,0:T(8,128)(2,1)}, bf16[128,1536]{1,0:T(8,128)(2,1)}, u32[]{:S(2)}, u32[]{:S(2)}) collective-permute-start(bf16[128,1536]{1,0:T(8,128)(2,1)} %pad_maximum_fusion.2), channel_id=1, source_target_pairs={{0,15},{1,0},{2,1},{3,2},{4,3},{5,4},{6,5},{7,6},{8,7},{9,8},{10,9... | collective-permute-start | bytes 1179656 | tf_op jit(solution)/shard_map/ppermute | solution.py:17
  24.7 0.8 pad_maximum_fusion.3
  25.5 3.3 %collective-permute-start.5 = (bf16[128,1536]{1,0:T(8,128)(2,1)}, bf16[128,1536]{1,0:T(8,128)(2,1)}, u32[]{:S(2)}, u32[]{:S(2)}) collective-permute-start(bf16[128,1536]{1,0:T(8,128)(2,1)} %pad_maximum_fusion.3), channel_id=1, source_target_pairs={{0,14},{1,3},{2,0},{3,5},{4,2},{5,7},{6,4},{7,9},{8,6},{9,11},{10,... | collective-permute-start | bytes 1179656 | tf_op jit(solution)/shard_map/ppermute | solution.py:23
  29.5 1.3 fusion.11
  30.8 11.8 %all-to-all-start = ((bf16[64,16,128]{2,1,0:T(8,128)(2,1)}), bf16[64,16,128]{2,1,0:T(8,128)(2,1)}, u32[]{:S(2)}, u32[]{:S(2)}) async-start(bf16[64,16,128]{2,1,0:T(8,128)(2,1)} %bitcast.10), calls=%async_computation | async-start | bytes 524288 | tf_op jit(solution)/shard_map/all_to_all | solution.py:74
  42.8 0.4 fusion.3
  43.2 1.8 fusion
  44.9 9.6 %all-to-all-done = bf16[64,16,128]{2,1,0:T(8,128)(2,1)} async-done(((bf16[64,16,128]{2,1,0:T(8,128)(2,1)}), bf16[64,16,128]{2,1,0:T(8,128)(2,1)}, u32[]{:S(2)}, u32[]{:S(2)}) %all-to-all-start) | async-done | bytes 262176 | tf_op jit(solution)/shard_map/all_to_all | solution.py:74
  54.5 1.6 fusion.93
  56.3 51.8 %all-gather.1 = f16[320,6144]{1,0:T(8,128)(2,1)S(1)} all-gather(f16[320,384]{1,0:T(8,128)(2,1)S(1)} %fusion.24), channel_id=1, replica_groups=mesh['dp'=64,'tensor'=16] {'tensor'}, dimensions={1}, use_global_device_ids=true | all-gather | bytes 4177920 | tf_op jit(solution)/shard_map/all_gather | solution.py:88
  108.1 1.2 multiply_convert_fusion
  109.3 1.9 collective-permute-start
  111.3 4.6 %collective-permute-start.1 = (bf16[320,128]{1,0:T(8,128)(2,1)S(1)}, bf16[320,128]{1,0:T(8,128)(2,1)S(1)}, u32[]{:S(2)}, u32[]{:S(2)}) collective-permute-start(bf16[320,128]{1,0:T(8,128)(2,1)S(1)} %multiply_convert_fusion), channel_id=1, source_target_pairs={{0,15},{1,0},{2,1},{3,2},{4,3},{5,4},{6,5},{7,6},{8,7},{9,8},{10,9... | collective-permute-start | bytes 245768 | tf_op jit(solution)/shard_map/ppermute | solution.py:17
  115.8 1.9 collective-permute-start.2
  117.8 3.5 %pad_maximum_fusion = bf16[512,1536]{1,0:T(8,128)(2,1)S(1)} fusion(bf16[128,1536]{1,0:T(8,128)(2,1)} %collective-permute-done.5, bf16[128,1536]{1,0:T(8,128)(2,1)} %collective-permute-done.4, bf16[128,1536]{1,0:T(8,128)(2,1)} %collective-permute-done.3, bf16[128,384]{1,0:T(8,128)(2,1)S(1)} %copy-done.3, bf16[128,384]{1,0:T(8,128)(2,1)S(1)} %copy-done.4, ...), kind=kLoop, calls=%fused_computation.6 | loop fusion | flops 11010048 | bytes 3145728 | tf_op jit(solution)/shard_map/concatenate | solution.py:93
  121.3 0.6 collective-permute-done.2
  122.3 3.9 %collective-permute-start.10 = (bf16[160,384]{1,0:T(8,128)(2,1)S(1)}, bf16[160,384]{1,0:T(8,128)(2,1)S(1)}, u32[]{:S(2)}, u32[]{:S(2)}) collective-permute-start(bf16[160,384]{1,0:T(8,128)(2,1)S(1)} %get-tuple-element.31), channel_id=1, source_target_pairs={{0,12},{1,13},{2,14},{3,15},{4,0},{5,1},{6,2},{7,3},{8,4},{9,5},{1... | collective-permute-start | bytes 368648 | tf_op jit(solution)/shard_map/ppermute | solution.py:17
  126.6 3.7 %collective-permute-start.6 = (bf16[160,384]{1,0:T(8,128)(2,1)S(1)}, bf16[160,384]{1,0:T(8,128)(2,1)S(1)}, u32[]{:S(2)}, u32[]{:S(2)}) collective-permute-start(bf16[160,384]{1,0:T(8,128)(2,1)S(1)} %slice.214), channel_id=1, source_target_pairs={{0,12},{1,13},{2,14},{3,15},{4,0},{5,1},{6,2},{7,3},{8,4},{9,5},{1... | collective-permute-start | bytes 368648 | tf_op jit(solution)/shard_map/ppermute | solution.py:17
  130.3 5.5 %collective-permute-start.7 = (bf16[160,384]{1,0:T(8,128)(2,1)S(1)}, bf16[160,384]{1,0:T(8,128)(2,1)S(1)}, u32[]{:S(2)}, u32[]{:S(2)}) collective-permute-start(bf16[160,384]{1,0:T(8,128)(2,1)S(1)} %get-tuple-element.30), channel_id=1, source_target_pairs={{0,4},{1,5},{2,6},{3,7},{4,8},{5,9},{6,10},{7,11},{8,12},{9,13},{1... | collective-permute-start | bytes 368648 | tf_op jit(solution)/shard_map/ppermute | solution.py:17
  136.2 5.3 %collective-permute-start.9 = (bf16[160,384]{1,0:T(8,128)(2,1)S(1)}, bf16[160,384]{1,0:T(8,128)(2,1)S(1)}, u32[]{:S(2)}, u32[]{:S(2)}) collective-permute-start(bf16[160,384]{1,0:T(8,128)(2,1)S(1)} %slice.213), channel_id=1, source_target_pairs={{0,4},{1,5},{2,6},{3,7},{4,8},{5,9},{6,10},{7,11},{8,12},{9,13},{1... | collective-permute-start | bytes 368648 | tf_op jit(solution)/shard_map/ppermute | solution.py:17
  141.5 3.9 %collective-permute-start.11 = (bf16[160,384]{1,0:T(8,128)(2,1)S(1)}, bf16[160,384]{1,0:T(8,128)(2,1)S(1)}, u32[]{:S(2)}, u32[]{:S(2)}) collective-permute-start(bf16[160,384]{1,0:T(8,128)(2,1)S(1)} %fusion.37), channel_id=1, source_target_pairs={{0,12},{1,13},{2,14},{3,15},{4,0},{5,1},{6,2},{7,3},{8,4},{9,5},{1... | collective-permute-start | bytes 368648 | tf_op jit(solution)/shard_map/ppermute | solution.py:17
  145.5 5.4 %collective-permute-start.8 = (bf16[160,384]{1,0:T(8,128)(2,1)S(1)}, bf16[160,384]{1,0:T(8,128)(2,1)S(1)}, u32[]{:S(2)}, u32[]{:S(2)}) collective-permute-start(bf16[160,384]{1,0:T(8,128)(2,1)S(1)} %fusion.40), channel_id=1, source_target_pairs={{0,4},{1,5},{2,6},{3,7},{4,8},{5,9},{6,10},{7,11},{8,12},{9,13},{1... | collective-permute-start | bytes 368648 | tf_op jit(solution)/shard_map/ppermute | solution.py:17
  151.2 6.2 %collective-permute-done.9 = bf16[160,384]{1,0:T(8,128)(2,1)S(1)} collective-permute-done((bf16[160,384]{1,0:T(8,128)(2,1)S(1)}, bf16[160,384]{1,0:T(8,128)(2,1)S(1)}, u32[]{:S(2)}, u32[]{:S(2)}) %collective-permute-start.9) | collective-permute-done | bytes 122912 | tf_op jit(solution)/shard_map/ppermute | solution.py:17
  157.4 11.4 %collective-permute-done.8 = bf16[160,384]{1,0:T(8,128)(2,1)S(1)} collective-permute-done((bf16[160,384]{1,0:T(8,128)(2,1)S(1)}, bf16[160,384]{1,0:T(8,128)(2,1)S(1)}, u32[]{:S(2)}, u32[]{:S(2)}) %collective-permute-start.8) | collective-permute-done | bytes 122912 | tf_op jit(solution)/shard_map/ppermute | solution.py:17
  168.9 1.4 convolution_convert_fusion
  170.3 10.2 %all-to-all-start.1 = ((bf16[64,16,128]{2,1,0:T(8,128)(2,1)}), bf16[64,16,128]{2,1,0:T(8,128)(2,1)S(1)}, u32[]{:S(2)}, u32[]{:S(2)}) async-start(bf16[64,16,128]{2,1,0:T(8,128)(2,1)} %bitcast.29), calls=%async_computation.1 | async-start | bytes 524288 | tf_op jit(solution)/shard_map/all_to_all | solution.py:124
  180.5 11.9 %all-to-all-done.1 = bf16[64,16,128]{2,1,0:T(8,128)(2,1)S(1)} async-done(((bf16[64,16,128]{2,1,0:T(8,128)(2,1)}), bf16[64,16,128]{2,1,0:T(8,128)(2,1)S(1)}, u32[]{:S(2)}, u32[]{:S(2)}) %all-to-all-start.1) | async-done | bytes 262176 | tf_op jit(solution)/shard_map/all_to_all | solution.py:124
  193.0 1.0 fusion.15
  (57 shorter events, 2.9 us)
Async XLA Ops:
  0.0 108.1 %copy-start = (bf16[1,6144,128]{2,1,0:T(8,128)(2,1)S(1)}, bf16[1,6144,128]{2,1,0:T(8,128)(2,1)}, u32[]{:S(2)}) copy-start(bf16[1,6144,128]{2,1,0:T(8,128)(2,1)} %param.8) | copy-start | bytes 4718596
  2.5 26.4 %copy-start.7 = (s32[128,2]{0,1:T(2,128)S(1)}, s32[128,2]{0,1:T(2,128)}, u32[]{:S(2)}) copy-start(s32[128,2]{0,1:T(2,128)} %param.6) | copy-start | bytes 3076
  2.5 26.6 %copy-start.6 = (bf16[128,384]{1,0:T(8,128)(2,1)S(1)}, bf16[128,384]{1,0:T(8,128)(2,1)}, u32[]{:S(2)}) copy-start(bf16[128,384]{1,0:T(8,128)(2,1)} %param.5) | copy-start | bytes 294916
  3.3 112.6 %collective-permute-start.3 = (bf16[128,1536]{1,0:T(8,128)(2,1)}, bf16[128,1536]{1,0:T(8,128)(2,1)}, u32[]{:S(2)}, u32[]{:S(2)}) collective-permute-start(bf16[128,1536]{1,0:T(8,128)(2,1)} %pad_maximum_fusion.1), channel_id=1, source_target_pairs={{0,1},{1,2},{2,3},{3,4},{4,5},{5,6},{6,7},{7,8},{8,9},{9,10},{10,1... | collective-permute-start | bytes 1179656 | tf_op jit(solution)/shard_map/ppermute | solution.py:17
  8.9 108.9 %collective-permute-start.4 = (bf16[128,1536]{1,0:T(8,128)(2,1)}, bf16[128,1536]{1,0:T(8,128)(2,1)}, u32[]{:S(2)}, u32[]{:S(2)}) collective-permute-start(bf16[128,1536]{1,0:T(8,128)(2,1)} %pad_maximum_fusion.2), channel_id=1, source_target_pairs={{0,15},{1,0},{2,1},{3,2},{4,3},{5,4},{6,5},{7,6},{8,7},{9,8},{10,9... | collective-permute-start | bytes 1179656 | tf_op jit(solution)/shard_map/ppermute | solution.py:17
  25.5 92.3 %collective-permute-start.5 = (bf16[128,1536]{1,0:T(8,128)(2,1)}, bf16[128,1536]{1,0:T(8,128)(2,1)}, u32[]{:S(2)}, u32[]{:S(2)}) collective-permute-start(bf16[128,1536]{1,0:T(8,128)(2,1)} %pad_maximum_fusion.3), channel_id=1, source_target_pairs={{0,14},{1,3},{2,0},{3,5},{4,2},{5,7},{6,4},{7,9},{8,6},{9,11},{10,... | collective-permute-start | bytes 1179656 | tf_op jit(solution)/shard_map/ppermute | solution.py:23
  30.8 23.7 %all-to-all-start = ((bf16[64,16,128]{2,1,0:T(8,128)(2,1)}), bf16[64,16,128]{2,1,0:T(8,128)(2,1)}, u32[]{:S(2)}, u32[]{:S(2)}) async-start(bf16[64,16,128]{2,1,0:T(8,128)(2,1)} %bitcast.10), calls=%async_computation | async-start | bytes 524288 | tf_op jit(solution)/shard_map/all_to_all | solution.py:74
  108.1 9.7 %copy-start.2 = (bf16[128,384]{1,0:T(8,128)(2,1)S(1)}, bf16[128,384]{1,0:T(8,128)(2,1)}, u32[]{:S(2)}) copy-start(bf16[128,384]{1,0:T(8,128)(2,1)} %get-tuple-element.7) | copy-start | bytes 294916
  108.1 9.7 %copy-start.3 = (bf16[128,384]{1,0:T(8,128)(2,1)S(1)}, bf16[128,384]{1,0:T(8,128)(2,1)}, u32[]{:S(2)}) copy-start(bf16[128,384]{1,0:T(8,128)(2,1)} %get-tuple-element.18) | copy-start | bytes 294916
  108.1 9.7 %copy-start.4 = (bf16[128,384]{1,0:T(8,128)(2,1)S(1)}, bf16[128,384]{1,0:T(8,128)(2,1)}, u32[]{:S(2)}) copy-start(bf16[128,384]{1,0:T(8,128)(2,1)} %get-tuple-element.19) | copy-start | bytes 294916
  108.1 9.7 %copy-start.5 = (bf16[128,384]{1,0:T(8,128)(2,1)S(1)}, bf16[128,384]{1,0:T(8,128)(2,1)}, u32[]{:S(2)}) copy-start(bf16[128,384]{1,0:T(8,128)(2,1)} %get-tuple-element.20) | copy-start | bytes 294916
  109.3 12.0 %collective-permute-start = (bf16[320,128]{1,0:T(8,128)(2,1)S(1)}, bf16[320,128]{1,0:T(8,128)(2,1)S(1)}, u32[]{:S(2)}, u32[]{:S(2)}) collective-permute-start(bf16[320,128]{1,0:T(8,128)(2,1)S(1)} %multiply_convert_fusion), channel_id=1, source_target_pairs={{0,1},{1,2},{2,3},{3,4},{4,5},{5,6},{6,7},{7,8},{8,9},{9,10},{10,1... | collective-permute-start | bytes 245768 | tf_op jit(solution)/shard_map/ppermute | solution.py:17
  111.3 10.1 %collective-permute-start.1 = (bf16[320,128]{1,0:T(8,128)(2,1)S(1)}, bf16[320,128]{1,0:T(8,128)(2,1)S(1)}, u32[]{:S(2)}, u32[]{:S(2)}) collective-permute-start(bf16[320,128]{1,0:T(8,128)(2,1)S(1)} %multiply_convert_fusion), channel_id=1, source_target_pairs={{0,15},{1,0},{2,1},{3,2},{4,3},{5,4},{6,5},{7,6},{8,7},{9,8},{10,9... | collective-permute-start | bytes 245768 | tf_op jit(solution)/shard_map/ppermute | solution.py:17
  115.8 6.1 %collective-permute-start.2 = (bf16[320,128]{1,0:T(8,128)(2,1)S(1)}, bf16[320,128]{1,0:T(8,128)(2,1)S(1)}, u32[]{:S(2)}, u32[]{:S(2)}) collective-permute-start(bf16[320,128]{1,0:T(8,128)(2,1)S(1)} %multiply_convert_fusion), channel_id=1, source_target_pairs={{0,14},{1,3},{2,0},{3,5},{4,2},{5,7},{6,4},{7,9},{8,6},{9,11},{10,... | collective-permute-start | bytes 245768 | tf_op jit(solution)/shard_map/ppermute | solution.py:23
  122.3 19.1 %collective-permute-start.10 = (bf16[160,384]{1,0:T(8,128)(2,1)S(1)}, bf16[160,384]{1,0:T(8,128)(2,1)S(1)}, u32[]{:S(2)}, u32[]{:S(2)}) collective-permute-start(bf16[160,384]{1,0:T(8,128)(2,1)S(1)} %get-tuple-element.31), channel_id=1, source_target_pairs={{0,12},{1,13},{2,14},{3,15},{4,0},{5,1},{6,2},{7,3},{8,4},{9,5},{1... | collective-permute-start | bytes 368648 | tf_op jit(solution)/shard_map/ppermute | solution.py:17
  126.6 24.7 %collective-permute-start.6 = (bf16[160,384]{1,0:T(8,128)(2,1)S(1)}, bf16[160,384]{1,0:T(8,128)(2,1)S(1)}, u32[]{:S(2)}, u32[]{:S(2)}) collective-permute-start(bf16[160,384]{1,0:T(8,128)(2,1)S(1)} %slice.214), channel_id=1, source_target_pairs={{0,12},{1,13},{2,14},{3,15},{4,0},{5,1},{6,2},{7,3},{8,4},{9,5},{1... | collective-permute-start | bytes 368648 | tf_op jit(solution)/shard_map/ppermute | solution.py:17
  130.3 15.2 %collective-permute-start.7 = (bf16[160,384]{1,0:T(8,128)(2,1)S(1)}, bf16[160,384]{1,0:T(8,128)(2,1)S(1)}, u32[]{:S(2)}, u32[]{:S(2)}) collective-permute-start(bf16[160,384]{1,0:T(8,128)(2,1)S(1)} %get-tuple-element.30), channel_id=1, source_target_pairs={{0,4},{1,5},{2,6},{3,7},{4,8},{5,9},{6,10},{7,11},{8,12},{9,13},{1... | collective-permute-start | bytes 368648 | tf_op jit(solution)/shard_map/ppermute | solution.py:17
  136.2 21.2 %collective-permute-start.9 = (bf16[160,384]{1,0:T(8,128)(2,1)S(1)}, bf16[160,384]{1,0:T(8,128)(2,1)S(1)}, u32[]{:S(2)}, u32[]{:S(2)}) collective-permute-start(bf16[160,384]{1,0:T(8,128)(2,1)S(1)} %slice.213), channel_id=1, source_target_pairs={{0,4},{1,5},{2,6},{3,7},{4,8},{5,9},{6,10},{7,11},{8,12},{9,13},{1... | collective-permute-start | bytes 368648 | tf_op jit(solution)/shard_map/ppermute | solution.py:17
  141.5 15.9 %collective-permute-start.11 = (bf16[160,384]{1,0:T(8,128)(2,1)S(1)}, bf16[160,384]{1,0:T(8,128)(2,1)S(1)}, u32[]{:S(2)}, u32[]{:S(2)}) collective-permute-start(bf16[160,384]{1,0:T(8,128)(2,1)S(1)} %fusion.37), channel_id=1, source_target_pairs={{0,12},{1,13},{2,14},{3,15},{4,0},{5,1},{6,2},{7,3},{8,4},{9,5},{1... | collective-permute-start | bytes 368648 | tf_op jit(solution)/shard_map/ppermute | solution.py:17
  145.5 23.4 %copy-start.1 = (bf16[1024,960]{1,0:T(8,128)(2,1)S(1)}, bf16[1024,960]{1,0:T(8,128)(2,1)}, u32[]{:S(2)}) copy-start(bf16[1024,960]{1,0:T(8,128)(2,1)} %fusion) | copy-start | bytes 5898244
  145.5 23.3 %collective-permute-start.8 = (bf16[160,384]{1,0:T(8,128)(2,1)S(1)}, bf16[160,384]{1,0:T(8,128)(2,1)S(1)}, u32[]{:S(2)}, u32[]{:S(2)}) collective-permute-start(bf16[160,384]{1,0:T(8,128)(2,1)S(1)} %fusion.40), channel_id=1, source_target_pairs={{0,4},{1,5},{2,6},{3,7},{4,8},{5,9},{6,10},{7,11},{8,12},{9,13},{1... | collective-permute-start | bytes 368648 | tf_op jit(solution)/shard_map/ppermute | solution.py:17
  168.9 11.6 %copy-start.8 = (f32[128,2]{0,1:T(2,128)S(1)}, f32[128,2]{0,1:T(2,128)}, u32[]{:S(2)}) copy-start(f32[128,2]{0,1:T(2,128)} %param.7) | copy-start | bytes 3076
  170.3 22.1 %all-to-all-start.1 = ((bf16[64,16,128]{2,1,0:T(8,128)(2,1)}), bf16[64,16,128]{2,1,0:T(8,128)(2,1)S(1)}, u32[]{:S(2)}, u32[]{:S(2)}) async-start(bf16[64,16,128]{2,1,0:T(8,128)(2,1)} %bitcast.29), calls=%async_computation.1 | async-start | bytes 524288 | tf_op jit(solution)/shard_map/all_to_all | solution.py:124
